TPU v7x, 32 devices: a whole 2x2x4 slice. The times are simulated.
32 devices in a mesh: dp: 8 (over y, x, core), tensor: 4 (over z).
Axes of the slice: x: 2, y: 2, z: 4, core: 2. Of those that a mesh axis runs over, the one named last changes fastest.
Arguments:
- memory: bfloat16 [12288, 1280], P('dp'), may hold values from -6 to 6
- hidden: bfloat16 [12288, 2560], P('dp', 'tensor'), may hold values from -6 to 6
- grad_out: bfloat16 [12288, 2560], P('dp', 'tensor'), may hold values from -6 to 6
- key_weight: bfloat16 [1280, 2560], P('dp', 'tensor'), may hold values from -0.15625 to 0.15625
- value_weight: bfloat16 [1280, 2560], P('dp', 'tensor'), may hold values from -0.15625 to 0.15625
- row_ids: int32 [12288, 5], P('dp'), may hold values from 0 to 65535, as said below
- embed_table: float32 [65536, 256], P(('dp', 'tensor')), may hold values from -6 to 6
- first_moment: float32 [65536, 256], P(('dp', 'tensor')), may hold values from -0.6 to 0.6
- second_moment: float32 [65536, 256], P(('dp', 'tensor')), may hold values from 0.001 to 0.1
Outputs:
- key_weight_grad: float32 [1280, 2560], P('dp', 'tensor')
- value_weight_grad: float32 [1280, 2560], P('dp', 'tensor')
- new_table: float32 [65536, 256], P(('dp', 'tensor'))
- new_first: float32 [65536, 256], P(('dp', 'tensor'))
- new_second: float32 [65536, 256], P(('dp', 'tensor'))
Inputs may be any that keep to these rules, and one draw needn't show every extreme that they name: `row_ids`: the table's rows fall into 32 owners of 2048 consecutive rows each. Taking the tokens in aligned blocks of 384 consecutive tokens with all their 5 ids, at most 180 ids of one block fall in one owner's rows, and in every block some owner gets exactly 180 of them.
All inputs are finite; a program needn't handle non-finite values.
Results may differ from a plain program's by a relative error of at most 0.0043.
Values may be sent and summed in bfloat16 or wider, within the bound.
A program may use at most 128 MiB of HBM per device.

v0:
```python
import math

import jax
import jax.numpy as jnp
from jax import lax
from jax.sharding import PartitionSpec as P

D = 2560


beta_one = 0.9
beta_two = 0.999
learn_rate = 0.01
adam_eps = 1e-08
norm_eps = 1e-06
correct_one = 0.9999734386011124
correct_two = 0.0952078528863


def adam_update(table_grad, embed_table, first_moment, second_moment):
    new_first = beta_one * first_moment + (1.0 - beta_one) * table_grad
    new_second = beta_two * second_moment + (1.0 - beta_two) * table_grad * table_grad
    stepped = new_first / correct_one / (jnp.sqrt(new_second / correct_two) + adam_eps)
    return (embed_table - learn_rate * stepped, new_first, new_second)


def body(
    memory,
    hidden,
    grad_out,
    key_weight,
    value_weight,
    row_ids,
    embed_table,
    first_moment,
    second_moment,
):
    key_full, value_full = (
        lax.all_gather(key_weight, "dp", axis=0, tiled=True),
        lax.all_gather(value_weight, "dp", axis=0, tiled=True),
    )
    key_proj = jnp.dot(memory, key_full, preferred_element_type=jnp.float32)
    value_proj = jnp.dot(memory, value_full, preferred_element_type=jnp.float32)
    hidden_float = hidden.astype(jnp.float32)
    grad_float = grad_out.astype(jnp.float32)
    root_width = math.sqrt(D)
    square_sum, cross_sum, output_sum = lax.psum(
        (
            jnp.sum(key_proj * key_proj, axis=1, keepdims=True),
            jnp.sum(hidden_float * key_proj, axis=1, keepdims=True),
            jnp.sum(grad_float * value_proj, axis=1, keepdims=True),
        ),
        "tensor",
    )
    key_scale = jnp.sqrt(square_sum / D + norm_eps)
    gate_score = cross_sum / (key_scale * root_width)
    gate_value = jax.nn.sigmoid(gate_score)
    gate_grad = gate_value * (1.0 - gate_value) * output_sum
    key_grad = gate_grad * (
        hidden_float / (key_scale * root_width)
        - gate_score * key_proj / (D * key_scale * key_scale)
    )
    value_grad = gate_value * grad_float
    both_grads = jnp.concatenate(
        [key_grad.astype(jnp.bfloat16), value_grad.astype(jnp.bfloat16)], axis=1
    )
    width_local = key_full.shape[1]
    dp_count = lax.axis_size("dp")
    tensor_count = lax.axis_size("tensor")
    weight_grads = lax.psum_scatter(
        lax.dot_general(
            memory, both_grads, (((0,), (0,)), ((), ())), preferred_element_type=jnp.float32
        ),
        "dp",
        scatter_dimension=0,
        tiled=True,
    )
    key_weight_grad = weight_grads[:, :width_local]
    value_weight_grad = weight_grads[:, width_local:]
    both_full = jnp.concatenate([key_full, value_full], axis=1)
    block_rows = memory.shape[0] // tensor_count
    memory_grad = lax.psum_scatter(
        lax.dot_general(
            both_grads, both_full, (((1,), (1,)), ((), ())), preferred_element_type=jnp.float32
        ),
        "tensor",
        scatter_dimension=0,
        tiled=True,
    ).astype(jnp.bfloat16)
    row_width = embed_table.shape[1]
    rows_dev = embed_table.shape[0]
    pieces = memory_grad.reshape(-1, row_width)
    entries = pieces.shape[0]
    my_ids = lax.dynamic_slice_in_dim(
        row_ids, lax.axis_index("tensor") * block_rows, block_rows, 0
    ).reshape(-1)
    owners = dp_count * tensor_count
    capacity = max(2, 3 * entries // owners)
    owner_of = my_ids // rows_dev
    local_row = my_ids % rows_dev
    owner_hits = (owner_of[:, None] == jnp.arange(owners, dtype=jnp.int32)[None, :]).astype(
        jnp.bfloat16
    )
    earlier = (jnp.arange(entries)[None, :] < jnp.arange(entries)[:, None]).astype(jnp.bfloat16)
    before_counts = jnp.dot(earlier, owner_hits, preferred_element_type=jnp.float32)
    slot_rank = jnp.sum(before_counts * owner_hits.astype(jnp.float32), axis=1).astype(jnp.int32)
    slot_index = owner_of * capacity + slot_rank
    send_rows = jnp.zeros((owners * capacity, row_width), jnp.bfloat16).at[slot_index].set(pieces)
    send_ids = jnp.full((owners * capacity,), rows_dev, jnp.int32).at[slot_index].set(local_row)
    got_rows, got_ids = (
        lax.all_to_all(
            send_rows.reshape(owners, capacity, row_width),
            ("dp", "tensor"),
            split_axis=0,
            concat_axis=0,
            tiled=True,
        ),
        lax.all_to_all(
            send_ids.reshape(owners, capacity),
            ("dp", "tensor"),
            split_axis=0,
            concat_axis=0,
            tiled=True,
        ),
    )
    table_grad = (
        jnp.zeros((rows_dev, row_width), jnp.float32)
        .at[got_ids.reshape(-1)]
        .add(got_rows.reshape(-1, row_width).astype(jnp.float32), mode="drop")
    )
    new_table, new_first, new_second = adam_update(
        table_grad, embed_table, first_moment, second_moment
    )
    return (key_weight_grad, value_weight_grad, new_table, new_first, new_second)


def solution(mesh):
    return jax.shard_map(
        body,
        mesh=mesh,
        in_specs=(
            P("dp", None),
            P("dp", "tensor"),
            P("dp", "tensor"),
            P("dp", "tensor"),
            P("dp", "tensor"),
            P("dp", None),
            P(("dp", "tensor"), None),
            P(("dp", "tensor"), None),
            P(("dp", "tensor"), None),
        ),
        out_specs=(
            P("dp", "tensor"),
            P("dp", "tensor"),
            P(("dp", "tensor"), None),
            P(("dp", "tensor"), None),
            P(("dp", "tensor"), None),
        ),
        check_vma=False,
    )
```

profile of v0, /device:TPU:0, one launch (start us, length us, event | category | flops | bytes accessed | tf_op | source)
XLA Modules:
  0.0 383.1 jit_solution(10919562007572725411)
XLA Ops:
  7.2 0.0 copy-start
  7.2 0.0 all-gather.5.cloned.1.call-start
  7.2 0.7 all-gather.5.cloned.1.call-update
  7.9 0.0 all-gather.3.cloned.1.call-start
  8.0 0.7 all-gather.3.cloned.1.call-update
  8.7 0.0 reduce-scatter.5.cloned.1.call-start
  8.7 2.7 copy.24
  11.4 4.0 %copy.25 = bf16[1536,640]{0,1:T(8,128)(2,1)} copy(bf16[1536,640]{1,0:T(8,128)(2,1)} %param.11) | data formatting | bytes 3932160 | tf_op args[2]
  15.4 23.1 %all-gather.5.cloned.1.call-done = bf16[1280,640]{1,0:T(8,128)(2,1)} async-done(((bf16[160,640]{1,0:T(8,128)(2,1)}), bf16[1280,640]{1,0:T(8,128)(2,1)}) %all-gather.5.cloned.1.call-update) | async-done | bytes 1638416 | tf_op jit(solution)/shard_map/all_gather | solution.py:40
  38.5 6.0 %fusion.5 = f32[1536]{0:T(1024)S(1)} fusion(bf16[1536,640]{0,1:T(8,128)(2,1)} %copy.25, bf16[1536,1280]{1,0:T(8,128)(2,1)} %param.9, bf16[1280,640]{1,0:T(8,128)(2,1)} %all-gather.5.cloned.1.call-done), kind=kOutput, calls=%fused_computation.14 | convolution fusion | flops 2519529984 | bytes 7542784 | tf_op jit(solution)/shard_map/dot_general | solution.py:43
  44.5 21.7 %all-gather.3.cloned.1.call-done = bf16[1280,640]{1,0:T(8,128)(2,1)} async-done(((bf16[160,640]{1,0:T(8,128)(2,1)}), bf16[1280,640]{1,0:T(8,128)(2,1)}) %all-gather.3.cloned.1.call-update) | async-done | bytes 1638416 | tf_op jit(solution)/shard_map/all_gather | solution.py:39
  66.2 7.6 %multiply_reduce_fusion = (f32[1536]{0:T(1024)S(1)}, f32[1536]{0:T(1024)S(1)}, f32[1536,640]{0,1:T(8,128)}) fusion(bf16[1536,640]{0,1:T(8,128)(2,1)S(1)} %copy.24, bf16[1536,1280]{1,0:T(8,128)(2,1)} %param.9, bf16[1280,640]{1,0:T(8,128)(2,1)} %all-gather.3.cloned.1.call-done), kind=kOutput, calls=%fused_computation.17 | convolution fusion | flops 2521494528 | bytes 11481088 | tf_op jit(solution)/shard_map/dot_general | solution.py:42
  73.8 18.9 %all-reduce = (f32[1536,1]{0,1:T(1,128)S(1)}, f32[1536,1]{0,1:T(1,128)S(1)}, f32[1536,1]{0,1:T(1,128)S(1)}) all-reduce(f32[1536,1]{0,1:T(1,128)S(1)} %broadcast_in_dim.24, f32[1536,1]{0,1:T(1,128)S(1)} %broadcast_in_dim.10, f32[1536,1]{0,1:T(1,128)S(1)} %broadcast_in_dim.11), channel_id=1, replica_groups=mesh['dp'=8,'tensor'=4] {'tensor'}, use_global_device_ids=true, to_apply=%region_5.0 | all-reduce | flops 4608 | bytes 36864 | tf_op jit(solution)/shard_map/psum | solution.py:47
  92.7 0.1 multiply_reduce_fusion.1
  92.8 0.1 fusion.27
  92.9 0.0 copy-start.4
  92.9 0.0 copy-start.5
  92.9 4.1 %fusion.4 = (bf16[1536,640]{0,1:T(8,128)(2,1)S(1)}, bf16[1536,640]{0,1:T(8,128)(2,1)S(1)}) fusion(bf16[1536,640]{0,1:T(8,128)(2,1)S(1)} %copy.24, f32[1536,640]{0,1:T(8,128)} %get-tuple-element.40, f32[1536]{0:T(1024)S(1)} %get-tuple-element.25, f32[1536]{0:T(1024)S(1)} %get-tuple-element.38, f32[1536]{0:T(1024)S(1)} %get-tuple-element.24, ...), kind=kLoop, calls=%fused_computation.13 | loop fusion | flops 9830400 | bytes 11827200 | tf_op jit(solution)/shard_map/convert_element_type | solution.py:65
  96.9 0.0 copy-start.1
  96.9 0.0 copy-start.3
  97.0 1.2 copy-done.1
  98.2 0.6 copy-done.3
  98.9 0.0 copy-done.4
  98.9 0.0 copy-done.5
  98.9 7.5 %fusion.7 = f32[1536,1280]{1,0:T(8,128)} fusion(bf16[1280,640]{1,0:T(8,128)(2,1)S(1)} %copy-done.4, bf16[1280,640]{1,0:T(8,128)(2,1)S(1)} %copy-done.5, bf16[1536,640]{0,1:T(8,128)(2,1)S(1)} %get-tuple-element.42, bf16[1536,640]{0,1:T(8,128)(2,1)S(1)} %get-tuple-element.41), kind=kOutput, calls=%fused_computation.18 | convolution fusion | flops 5047582720 | bytes 15073280 | tf_op jit(solution)/shard_map/dot_general | solution.py:83
  106.3 0.0 copy-start.2
  106.3 0.0 reduce-scatter.5.cloned.1.call-update
  106.4 0.2 reduce-scatter.7.cloned.1.call-start
  106.6 1.3 copy-done.2
  107.9 10.3 %convolution_bitcast_fusion = f32[1280,1280]{0,1:T(8,128)} fusion(bf16[1536,1280]{1,0:T(8,128)(2,1)} %param.9, bf16[1536,640]{0,1:T(8,128)(2,1)} %copy-done.3, bf16[1536,640]{0,1:T(8,128)(2,1)S(1)} %copy-done.2), kind=kOutput, calls=%fused_computation.5 | convolution fusion | flops 5041029120 | bytes 14417920 | tf_op jit(solution)/shard_map/dot_general | solution.py:71
  118.1 8.2 %copy.30 = f32[1280,1280]{1,0:T(8,128)} copy(f32[1280,1280]{0,1:T(8,128)} %convolution_bitcast_fusion) | data formatting | bytes 13107200
  126.3 0.0 reduce-scatter.7.cloned.1.call-update
  126.3 0.0 copy-done
  126.3 0.1 copy.26
  126.5 0.2 reshape.162
  126.7 0.2 reshape.163
  126.9 1.4 fusion.15
  128.3 0.1 fusion.24
  128.4 10.0 %scatter_custom_fusion = s32[5760]{0:T(1024)S(1)} fusion(s32[1920]{0:T(1024)S(1)} %fusion.24, s32[1920]{0:T(1024)S(1)} %get-tuple-element.36, s32[]{:T(128)} %constant.22.clone.1), kind=kCustom, calls=%fused_computation.47 | custom fusion | bytes 23044 | tf_op jit(solution)/shard_map/scatter | solution.py:109
  138.4 0.8 all_to_all.9
  139.2 2.6 all-to-all-start
  141.8 98.8 %reduce-scatter.5.cloned.1.call-done = f32[384,1280]{1,0:T(8,128)} async-done(((f32[1536,1280]{1,0:T(8,128)}), f32[384,1280]{1,0:T(8,128)}) %reduce-scatter.5.cloned.1.call-update) | async-done | bytes 1966096 | tf_op jit(solution)/shard_map/reduce_scatter | solution.py:82
  240.6 1.6 convert_element_type.49
  242.2 1.6 reshape.180
  243.9 11.8 %scatter_custom_fusion.1 = bf16[5760,256]{1,0:T(8,128)(2,1)S(1)} fusion(s32[1920]{0:T(1024)S(1)} %fusion.24, bf16[1920,256]{1,0:T(8,128)(2,1)} %reshape.180, bf16[]{:T(256)} %constant.69.clone.1), kind=kCustom, calls=%fused_computation.27 | custom fusion | bytes 2949632 | tf_op jit(solution)/shard_map/scatter | solution.py:108
  255.7 2.3 reshape.166
  258.0 0.0 all-to-all-done
  258.0 5.3 %all-to-all-start.1 = ((bf16[32,180,256]{2,1,0:T(8,128)(2,1)}), bf16[32,180,256]{2,1,0:T(8,128)(2,1)S(1)}, u32[]{:S(2)}, u32[]{:S(2)}) async-start(bf16[32,180,256]{2,1,0:T(8,128)(2,1)} %reshape.166), calls=%async_computation.2 | async-start | bytes 6029312 | tf_op jit(solution)/shard_map/all_to_all | solution.py:111
  263.3 0.1 reduce.6
  263.4 0.2 reshape.164
  263.5 0.1 fusion.20
  263.6 70.3 %reduce-scatter.7.cloned.1.call-done = f32[160,1280]{1,0:T(8,128)} async-done(((f32[1280,1280]{1,0:T(8,128)}), f32[160,1280]{1,0:T(8,128)}) %reduce-scatter.7.cloned.1.call-update) | async-done | bytes 819216
  333.9 2.1 fusion.33
  335.9 0.0 all-to-all-done.1
  335.9 3.0 reshape.188
  339.0 31.2 %scatter_custom_fusion.2 = f32[2048,256]{1,0:T(8,128)S(1)} fusion(s32[5760]{0:T(1024)S(1)} %fusion.20, f32[5760,256]{1,0:T(8,128)} %reshape.188, f32[]{:T(128)} %constant.27.clone.1), kind=kCustom, calls=%fused_computation.30 | custom fusion | flops 1474560 | bytes 2097664 | tf_op jit(solution)/shard_map/scatter-add | solution.py:129
  370.2 6.4 %multiply_subtract_fusion = (f32[2048,256]{1,0:T(8,128)}, f32[2048,256]{1,0:T(8,128)}, f32[2048,256]{1,0:T(8,128)}) fusion(f32[2048,256]{1,0:T(8,128)} %param.15, f32[2048,256]{1,0:T(8,128)S(1)} %scatter_custom_fusion.2, f32[2048,256]{1,0:T(8,128)} %param.16, f32[2048,256]{1,0:T(8,128)} %param.17), kind=kLoop, calls=%fused_computation.25 | loop fusion | flops 6815744 | bytes 14680064 | tf_op jit(solution)/shard_map/sub | solution.py:24
  (6 shorter events, 0.0 us)
Async XLA Ops:
  7.2 119.1 %copy-start = (s32[1536,5]{0,1:T(8,128)S(1)}, s32[1536,5]{0,1:T(8,128)}, u32[]{:S(2)}) copy-start(s32[1536,5]{0,1:T(8,128)} %param.14) | copy-start | bytes 92164
  7.2 31.3 %all-gather.5.cloned.1.call-start = ((), (), s32[]{:S(2)}) async-start(), calls=%async_computation.5 | async-start | bytes 1843200 | tf_op jit(solution)/shard_map/all_gather | solution.py:40
  7.9 58.3 %all-gather.3.cloned.1.call-start = ((), (), s32[]{:S(2)}) async-start(), calls=%async_computation.4 | async-start | bytes 1843200 | tf_op jit(solution)/shard_map/all_gather | solution.py:39
  8.7 231.9 %reduce-scatter.5.cloned.1.call-start = ((), (), s32[]{:S(2)}) async-start(), calls=%async_computation.6 | async-start | bytes 9830400 | tf_op jit(solution)/shard_map/reduce_scatter | solution.py:82
  92.9 6.0 %copy-start.4 = (bf16[1280,640]{1,0:T(8,128)(2,1)S(1)}, bf16[1280,640]{1,0:T(8,128)(2,1)}, u32[]{:S(2)}) copy-start(bf16[1280,640]{1,0:T(8,128)(2,1)} %all-gather.5.cloned.1.call-done) | copy-start | bytes 4915204
  92.9 6.0 %copy-start.5 = (bf16[1280,640]{1,0:T(8,128)(2,1)S(1)}, bf16[1280,640]{1,0:T(8,128)(2,1)}, u32[]{:S(2)}) copy-start(bf16[1280,640]{1,0:T(8,128)(2,1)} %all-gather.3.cloned.1.call-done) | copy-start | bytes 4915204
  96.9 1.3 copy-start.1
  96.9 1.9 copy-start.3
  106.3 1.5 copy-start.2
  106.4 227.5 %reduce-scatter.7.cloned.1.call-start = ((), (), s32[]{:S(2)}) async-start(), calls=%async_computation.7 | async-start | bytes 7372800
  139.2 118.8 %all-to-all-start = ((s32[32,1,180]{2,1,0:T(1,128)}), s32[32,1,180]{2,1,0:T(1,128)S(1)}, u32[]{:S(2)}, u32[]{:S(2)}) async-start(s32[32,1,180]{2,1,0:T(1,128)} %all_to_all.9), calls=%async_computation | async-start | bytes 65536 | tf_op jit(solution)/shard_map/all_to_all | solution.py:118
  258.0 78.0 %all-to-all-start.1 = ((bf16[32,180,256]{2,1,0:T(8,128)(2,1)}), bf16[32,180,256]{2,1,0:T(8,128)(2,1)S(1)}, u32[]{:S(2)}, u32[]{:S(2)}) async-start(bf16[32,180,256]{2,1,0:T(8,128)(2,1)} %reshape.166), calls=%async_computation.2 | async-start | bytes 6029312 | tf_op jit(solution)/shard_map/all_to_all | solution.py:111
Sparse Core Ops, SparseCore 0:
  9.9 28.5 all-gather.4
  40.4 25.8 all-gather.2
  106.5 134.0 reduce-scatter.4
  243.9 89.9 reduce-scatter.6
where the time goes:
time: 384 us; the launch traced here: 383 us
  waiting for transfers between devices  215 us (56%)
  local copies, waits for them, and re-layouts  50.4 us (13%)
  other arithmetic  43.6 us (11%)
  matrix products  32.7 us (9%)
  blocking collectives  18.9 us (5%)
  between operations  14 us (4%)
  starting transfers between devices  8.23 us (2%)
    reduce_scatter x1, waiting for transfers between devices, body(): lax.psum_scatter(lax.dot_general(both_grads, both_full, (((1,), (1,)), ((...  98.8 us
    unnamed x5, waiting for transfers between devices  71.7 us
    scatter-add x1, other arithmetic, body(): table_grad = jnp.zeros((rows_dev, row_width), jnp.float32).at[got_ids.res...  31.2 us
    all_gather x1, waiting for transfers between devices, body(): lax.all_gather(value_weight, 'dp', axis=0, tiled=True)  23.1 us
    all_gather x1, waiting for transfers between devices, body(): lax.all_gather(key_weight, 'dp', axis=0, tiled=True)  21.7 us
    psum x1, blocking collectives, body(): lax.psum((jnp.sum(key_proj * key_proj, axis=1, keepdims=True), jnp.sum(hi...  18.9 us
    unnamed x15, local copies, waits for them, and re-layouts  18 us
    scatter x1, local copies, waits for them, and re-layouts, body(): jnp.zeros((owners * capacity, row_width), jnp.bfloat16).at[slot_index]  11.8 us
  transfers between devices with their start and end apart: 6, of which 4 were waited for; matrix products, arithmetic and copies ran while one was open for 16% of the time, Pallas kernels for 0%

commit v1 on v0

v1 whole, which is shorter than its diff:
```python
import math

import jax
import jax.numpy as jnp
from jax import lax
from jax.experimental import pallas as pl
from jax.experimental.pallas import tpu as pltpu
from jax.sharding import PartitionSpec as P

beta_one = 0.9
beta_two = 0.999
learn_rate = 0.01
adam_eps = 1e-08
norm_eps = 1e-06
correct_one = 0.9999734386011124
correct_two = 0.0952078528863


def adam_update(table_grad, embed_table, first_moment, second_moment):
    new_first = beta_one * first_moment + (1.0 - beta_one) * table_grad
    new_second = beta_two * second_moment + (1.0 - beta_two) * table_grad * table_grad
    stepped = new_first / correct_one / (jnp.sqrt(new_second / correct_two) + adam_eps)
    return (embed_table - learn_rate * stepped, new_first, new_second)


f32 = jnp.float32
bf16 = jnp.bfloat16
lanes = 128
sublanes = 8


def full_spec(shape):
    return pl.BlockSpec(shape, lambda i: (0,) * len(shape))


def project_kernel(memory_ref, weights_ref, hidden_ref, grad_ref, key_ref, sums_ref):
    width = hidden_ref.shape[1]
    tile = memory_ref.shape[0]
    proj = jnp.dot(memory_ref[...], weights_ref[...], preferred_element_type=f32)
    key_proj = proj[:, :width]
    key_ref[...] = key_proj
    square = jnp.sum(key_proj * key_proj, axis=1, keepdims=True)
    cross = jnp.sum(hidden_ref[...].astype(f32) * key_proj, axis=1, keepdims=True)
    output = jnp.sum(grad_ref[...].astype(f32) * proj[:, width:], axis=1, keepdims=True)
    lane = lax.broadcasted_iota(jnp.int32, (tile, lanes), 1)
    packed = jnp.where(
        lane == 0, square, jnp.where(lane == 1, cross, jnp.where(lane == 2, output, 0.0))
    )
    sums_ref[...] = packed.T[:sublanes, :]


def grads_kernel(
    model_width, sums_ref, hidden_ref, grad_ref, key_ref, weights_ref, both_ref, piece_ref
):
    width = hidden_ref.shape[1]
    tile = hidden_ref.shape[0]
    sums = sums_ref[0]
    for part in range(1, sums_ref.shape[0]):
        sums = sums + sums_ref[part]
    root_width = math.sqrt(model_width)
    key_scale = jnp.sqrt(sums[0:1] / model_width + norm_eps)
    gate_score = sums[1:2] / (key_scale * root_width)
    gate_value = 1.0 / (1.0 + jnp.exp(-gate_score))
    gate_grad = gate_value * (1.0 - gate_value) * sums[2:3]
    hidden_factor = gate_grad / (key_scale * root_width)
    key_factor = gate_grad * (gate_score / (model_width * key_scale * key_scale))
    row = lax.broadcasted_iota(jnp.int32, (lanes, tile), 0)
    factors = jnp.where(
        row == 0, hidden_factor, jnp.where(row == 1, key_factor, gate_value)
    ).T
    key_grad = (
        factors[:, 0:1] * hidden_ref[...].astype(f32) - factors[:, 1:2] * key_ref[...]
    ).astype(bf16)
    value_grad = (factors[:, 2:3] * grad_ref[...].astype(f32)).astype(bf16)
    both_ref[:, :width] = key_grad
    both_ref[:, width:] = value_grad
    contract = (((1,), (1,)), ((), ()))
    piece_ref[...] = lax.dot_general(
        both_ref[...], weights_ref[...], contract, preferred_element_type=f32
    ).astype(bf16)


def dispatch_kernel(lookups, row_width, slot_ref, total_ref, out_ref):
    block = total_ref.shape[0]
    tile = out_ref.shape[0]
    slot = lax.broadcasted_iota(jnp.int32, (tile, block), 0) + pl.program_id(0) * tile
    rows = jnp.zeros((tile, row_width), f32)
    for lookup in range(lookups):
        hot = jnp.where(slot == slot_ref[:, lookup * block : (lookup + 1) * block], 1.0, 0.0)
        rows = rows + jnp.dot(
            hot.astype(bf16),
            total_ref[:, lookup * row_width : (lookup + 1) * row_width],
            preferred_element_type=f32,
        )
    out_ref[...] = rows.astype(bf16)


def combine_kernel(
    chunk, ids_ref, rows_ref, table_ref, first_ref, second_ref, new_table, new_first, new_second
):
    tile, row_width = table_ref.shape
    row = lax.broadcasted_iota(jnp.int32, (tile, chunk), 0) + pl.program_id(0) * tile
    table_grad = jnp.zeros((tile, row_width), f32)
    for start in range(0, rows_ref.shape[0], chunk):
        hot = jnp.where(row == ids_ref[:, start : start + chunk], 1.0, 0.0)
        table_grad = table_grad + jnp.dot(
            hot.astype(bf16), rows_ref[start : start + chunk, :], preferred_element_type=f32
        )
    new_table[...], new_first[...], new_second[...] = adam_update(
        table_grad, table_ref[...], first_ref[...], second_ref[...]
    )


def divisor(count, choices):
    return next((c for c in choices if count % c == 0), count)


def body(
    memory,
    hidden,
    grad_out,
    key_weight,
    value_weight,
    row_ids,
    embed_table,
    first_moment,
    second_moment,
):
    dp_count = lax.axis_size("dp")
    tensor_count = lax.axis_size("tensor")
    tokens, mem = memory.shape
    width = hidden.shape[1]
    model_width = width * tensor_count
    rows_dev, row_width = embed_table.shape
    lookups = row_ids.shape[1]
    block = tokens // tensor_count
    entries = block * lookups
    owners = dp_count * tensor_count
    capacity = max(2, 3 * entries // owners)
    slots = owners * capacity

    weights = lax.all_gather(
        jnp.concatenate([key_weight, value_weight], axis=1), "dp", axis=0, tiled=True
    )

    my_ids = lax.dynamic_slice_in_dim(row_ids, lax.axis_index("tensor") * block, block, 0)
    my_ids = my_ids.T.reshape(-1)
    owner_of = my_ids // rows_dev
    local_row = my_ids % rows_dev
    owner_hits = (owner_of[:, None] == jnp.arange(owners, dtype=jnp.int32)[None, :]).astype(bf16)
    earlier = (jnp.arange(entries)[None, :] < jnp.arange(entries)[:, None]).astype(bf16)
    before_counts = jnp.dot(earlier, owner_hits, preferred_element_type=f32)
    slot_rank = jnp.sum(before_counts * owner_hits.astype(f32), axis=1).astype(jnp.int32)
    slot_index = owner_of * capacity + slot_rank
    rank_hits = slot_rank[:, None] == jnp.arange(capacity, dtype=jnp.int32)[None, :]
    code = local_row + 1
    coded = jnp.concatenate(
        [
            jnp.where(rank_hits, (code // 64)[:, None], 0),
            jnp.where(rank_hits, (code % 64)[:, None], 0),
        ],
        axis=1,
    ).astype(bf16)
    sent_codes = lax.dot_general(
        owner_hits, coded, (((0,), (0,)), ((), ())), preferred_element_type=f32
    ).astype(jnp.int32)
    send_ids = sent_codes[:, :capacity] * 64 + sent_codes[:, capacity:] - 1
    got_ids = lax.all_to_all(
        send_ids, ("dp", "tensor"), split_axis=0, concat_axis=0, tiled=True
    ).reshape(1, slots)

    tile = divisor(tokens, (256, 128))
    steps = tokens // tile
    token_spec = lambda columns: pl.BlockSpec((tile, columns), lambda i: (i, 0))
    key_proj, sums = pl.pallas_call(
        project_kernel,
        grid=(steps,),
        in_specs=[token_spec(mem), full_spec((mem, 2 * width)), token_spec(width), token_spec(width)],
        out_specs=[token_spec(width), pl.BlockSpec((sublanes, tile), lambda i: (0, i))],
        out_shape=[
            jax.ShapeDtypeStruct((tokens, width), f32),
            jax.ShapeDtypeStruct((sublanes, tokens), f32),
        ],
        cost_estimate=pl.CostEstimate(
            flops=4 * tokens * mem * width, bytes_accessed=12 * tokens * width, transcendentals=0
        ),
        name="project",
    )(memory, weights, hidden, grad_out)
    all_sums = lax.all_gather(sums, "tensor", axis=0)
    both_grads, pieces = pl.pallas_call(
        lambda *refs: grads_kernel(model_width, *refs),
        grid=(steps,),
        in_specs=[
            pl.BlockSpec((tensor_count, sublanes, tile), lambda i: (0, 0, i)),
            token_spec(width),
            token_spec(width),
            token_spec(width),
            full_spec((mem, 2 * width)),
        ],
        out_specs=[token_spec(2 * width), token_spec(mem)],
        out_shape=[
            jax.ShapeDtypeStruct((tokens, 2 * width), bf16),
            jax.ShapeDtypeStruct((tokens, mem), bf16),
        ],
        cost_estimate=pl.CostEstimate(
            flops=4 * tokens * mem * width, bytes_accessed=16 * tokens * width, transcendentals=0
        ),
        name="grads",
    )(all_sums, hidden, grad_out, key_proj, weights)
    total = lax.psum_scatter(pieces, "tensor", scatter_dimension=0, tiled=True)
    weight_grads = lax.psum_scatter(
        lax.dot_general(
            memory, both_grads, (((0,), (0,)), ((), ())), preferred_element_type=f32
        ).astype(bf16),
        "dp",
        scatter_dimension=0,
        tiled=True,
    ).astype(f32)

    slot_tile = divisor(slots, (720, 960, 640, 128))
    send_rows = pl.pallas_call(
        lambda *refs: dispatch_kernel(lookups, row_width, *refs),
        grid=(slots // slot_tile,),
        in_specs=[full_spec((1, entries)), full_spec((block, mem))],
        out_specs=pl.BlockSpec((slot_tile, row_width), lambda i: (i, 0)),
        out_shape=jax.ShapeDtypeStruct((slots, row_width), bf16),
        cost_estimate=pl.CostEstimate(
            flops=2 * slots * entries * row_width, bytes_accessed=4 * slots * row_width,
            transcendentals=0,
        ),
        name="dispatch",
    )(slot_index.reshape(1, entries), total)
    got_rows = lax.all_to_all(
        send_rows.reshape(owners, capacity, row_width),
        ("dp", "tensor"),
        split_axis=0,
        concat_axis=0,
        tiled=True,
    ).reshape(slots, row_width)
    row_tile = divisor(rows_dev, (256, 128))
    row_spec = pl.BlockSpec((row_tile, row_width), lambda i: (i, 0))
    table_shape = jax.ShapeDtypeStruct((rows_dev, row_width), f32)
    chunk = divisor(slots, (1152, 960, 640, 128))
    new_table, new_first, new_second = pl.pallas_call(
        lambda *refs: combine_kernel(chunk, *refs),
        grid=(rows_dev // row_tile,),
        in_specs=[full_spec((1, slots)), full_spec((slots, row_width)), row_spec, row_spec, row_spec],
        out_specs=[row_spec] * 3,
        out_shape=[table_shape] * 3,
        cost_estimate=pl.CostEstimate(
            flops=2 * slots * rows_dev * row_width, bytes_accessed=24 * rows_dev * row_width,
            transcendentals=0,
        ),
        name="combine",
    )(got_ids, got_rows, embed_table, first_moment, second_moment)
    return (weight_grads[:, :width], weight_grads[:, width:], new_table, new_first, new_second)


def solution(mesh):
    return jax.shard_map(
        body,
        mesh=mesh,
        in_specs=(
            P("dp", None),
            P("dp", "tensor"),
            P("dp", "tensor"),
            P("dp", "tensor"),
            P("dp", "tensor"),
            P("dp", None),
            P(("dp", "tensor"), None),
            P(("dp", "tensor"), None),
            P(("dp", "tensor"), None),
        ),
        out_specs=(
            P("dp", "tensor"),
            P("dp", "tensor"),
            P(("dp", "tensor"), None),
            P(("dp", "tensor"), None),
            P(("dp", "tensor"), None),
        ),
        check_vma=False,
    )
```

time: 384 us -> 279 us (0.73)
  waiting for transfers between devices: 215 us -> 154 us
  Pallas kernels: 0 us -> 46.3 us
  other arithmetic: 43.6 us -> 4.05 us
  local copies, waits for them, and re-layouts: 50.4 us -> 23.8 us
  matrix products: 32.7 us -> 11.5 us
    pallas_call x0 -> x4, Pallas kernels: none -> 46.3 us  [the longest x1 13.1 us: body(): pl.pallas_call(lambda *refs: combine_kernel(chunk, *refs), grid=(rows_dev...]
    reduce_scatter x1, waiting for transfers between devices: 98.8 us -> 63.1 us  [body(): total = lax.psum_scatter(pieces, 'tensor', scatter_dimension=0, tiled=True)]
    scatter-add x1 -> x0, other arithmetic: 31.2 us -> none  [body(): table_grad = jnp.zeros((rows_dev, row_width), jnp.float32).at[got_ids.res...]
    scatter x2 -> x0, local copies, waits for them, and re-layouts: 21.8 us -> none  [the longest x1 11.8 us: body(): jnp.zeros((owners * capacity, row_width), jnp.bfloat16).at[slot_index]]
    dot_general x4 -> x2, matrix products: 22.4 us -> 1.98 us  [the longest x1 1.38 us: body(): before_counts = jnp.dot(earlier, owner_hits, preferred_element_type=f32)]
    psum x1 -> x0, blocking collectives: 18.9 us -> none  [body(): lax.psum((jnp.sum(key_proj * key_proj, axis=1, keepdims=True), jnp.sum(hi...]
    unnamed x5 -> x4, waiting for transfers between devices: 71.7 us -> 54.5 us
    all_gather x0 -> x1, blocking collectives: none -> 15.5 us  [body(): all_sums = lax.all_gather(sums, 'tensor', axis=0)]
  transfers between devices with their start and end apart: 6 -> 5, of which waited for: 4 -> 3; matrix products, arithmetic and copies ran while one was open for 16% -> 13% of each run, Pallas kernels for 0% -> 4%
where the time goes in v1:
time: 279 us; the launch traced here: 278 us
  waiting for transfers between devices  154 us (55%)
  Pallas kernels  46.3 us (17%)
  local copies, waits for them, and re-layouts  23.8 us (9%)
  blocking collectives  15.5 us (6%)
  between operations  13.8 us (5%)
  matrix products  11.5 us (4%)
  starting transfers between devices  8.94 us (3%)
  other arithmetic  4.05 us (1%)
    reduce_scatter x1, waiting for transfers between devices, body(): total = lax.psum_scatter(pieces, 'tensor', scatter_dimension=0, tiled=True)  63.1 us
    unnamed x4, waiting for transfers between devices  54.5 us
    all_gather x1, waiting for transfers between devices, body(): lax.all_gather(jnp.concatenate([key_weight, value_weight], axis=1), 'dp',...  36.8 us
    all_gather x1, blocking collectives, body(): all_sums = lax.all_gather(sums, 'tensor', axis=0)  15.5 us
    pallas_call x1, Pallas kernels, body(): pl.pallas_call(lambda *refs: combine_kernel(chunk, *refs), grid=(rows_dev...  13.1 us
    unnamed x6, local copies, waits for them, and re-layouts  12.6 us
    pallas_call x1, Pallas kernels, body(): pl.pallas_call(lambda *refs: grads_kernel(model_width, *refs), grid=(step...  12.1 us
    pallas_call x1, Pallas kernels, body(): pl.pallas_call(lambda *refs: dispatch_kernel(lookups, row_width, *refs),...  10.9 us
  transfers between devices with their start and end apart: 5, of which 3 were waited for; matrix products, arithmetic and copies ran while one was open for 13% of the time, Pallas kernels for 4%

profile of v1, /device:TPU:0, one launch (start us, length us, event | category | flops | bytes accessed | tf_op | source)
XLA Modules:
  0.0 278.3 jit_solution(15832017212851247458)
XLA Ops:
  7.2 0.0 all-gather.3.cloned.1.call-start
  7.2 1.8 pad_maximum_fusion
  9.0 0.0 all-gather.3.cloned.1.call-update
  9.0 0.0 reduce-scatter.5.cloned.1.call-start
  9.1 36.8 %all-gather.3.cloned.1.call-done.weights_ref.refs_4_ = bf16[1280,1280]{1,0:T(8,128)(2,1)} async-done(((bf16[160,1280]{1,0:T(8,128)(2,1)}), bf16[1280,1280]{1,0:T(8,128)(2,1)}) %all-gather.3.cloned.1.call-update) | async-done | bytes 3276816 | tf_op jit(solution)/shard_map/all_gather | solution.py:142
  45.9 10.2 %project.1 = (f32[1536,640]{1,0:T(8,128)}, f32[8,1536]{1,0:T(8,128)}) custom-call(bf16[1536,1280]{1,0:T(8,128)(2,1)} %memory_ref.1, bf16[1280,1280]{1,0:T(8,128)(2,1)} %all-gather.3.cloned.1.call-done.weights_ref.refs_4_, bf16[1536,640]{1,0:T(8,128)(2,1)} %refs_1_.1, bf16[1536,640]{1,0:T(8,128)(2,1)} %refs_2_.2), custom_call_target="tpu_custom_call" | custom-call | flops 5033164800 | bytes 11796480 | tf_op jit(solution)/shard_map/project/pallas_call | solution.py:175
  56.1 15.5 %all-gather = f32[32,1536]{1,0:T(8,128)} all-gather(f32[8,1536]{1,0:T(8,128)} %get-tuple-element.12), channel_id=2, replica_groups=mesh['dp'=8,'tensor'=4] {'tensor'}, dimensions={0}, use_global_device_ids=true | all-gather | bytes 245760 | tf_op jit(solution)/shard_map/all_gather | solution.py:189
  71.6 12.1 %grads.1 = (bf16[1536,1280]{1,0:T(8,128)(2,1)}, bf16[1536,1280]{1,0:T(8,128)(2,1)}) custom-call(f32[4,8,1536]{2,1,0:T(8,128)} %bitcast.14, bf16[1536,640]{1,0:T(8,128)(2,1)} %refs_1_.1, bf16[1536,640]{1,0:T(8,128)(2,1)} %refs_2_.2, f32[1536,640]{1,0:T(8,128)} %get-tuple-element.13.refs_3_, bf16[1280,1280]{1,0:T(8,128)(2,1)} %all-gather.3.cloned.1.call-done.weights_ref.refs_4_), custom_call_target="tpu_custom_call" | custom-call | flops 5033164800 | bytes 15728640 | tf_op jit(solution)/shard_map/grads/pallas_call | solution.py:190
  83.7 0.0 reduce-scatter.5.cloned.1.call-update
  83.7 0.7 dynamic-slice_bitcast_fusion
  84.5 1.4 fusion.7
  85.9 1.4 select_convert_fusion.1
  87.3 0.6 fusion.8
  87.9 0.1 fusion.15
  88.0 0.7 copy.18
  88.6 3.7 %all-to-all-start = ((s32[32,1,180]{2,1,0:T(1,128)}), s32[32,1,180]{2,1,0:T(1,128)S(1)}, u32[]{:S(2)}, u32[]{:S(2)}) async-start(s32[32,1,180]{2,1,0:T(1,128)} %copy.18), calls=%async_computation | async-start | bytes 65536 | tf_op jit(solution)/shard_map/all_to_all | solution.py:168
  92.4 0.6 reshape_add_fusion.refs_0_
  93.0 63.1 %reduce-scatter.5.cloned.1.call-done.refs_1_ = bf16[384,1280]{1,0:T(8,128)(2,1)} async-done(((bf16[1536,1280]{1,0:T(8,128)(2,1)}), bf16[384,1280]{1,0:T(8,128)(2,1)}) %reduce-scatter.5.cloned.1.call-update) | async-done | bytes 983056 | tf_op jit(solution)/shard_map/reduce_scatter | solution.py:210
  156.1 10.9 %dispatch.1 = bf16[5760,256]{1,0:T(8,128)(2,1)} custom-call(s32[1,1920]{1,0:T(1,128)} %reshape_add_fusion.refs_0_, bf16[384,1280]{1,0:T(8,128)(2,1)} %reduce-scatter.5.cloned.1.call-done.refs_1_), custom_call_target="tpu_custom_call" | custom-call | flops 5662310400 | bytes 5898240 | tf_op jit(solution)/shard_map/dispatch/pallas_call | solution.py:221
  167.0 5.3 %reshape.201 = bf16[32,180,256]{2,1,0:T(8,128)(2,1)} reshape(bf16[5760,256]{1,0:T(8,128)(2,1)} %dispatch.1) | data formatting | bytes 5898240 | tf_op jit(solution)/shard_map/reshape | solution.py:234
  172.3 0.0 all-to-all-done
  172.3 5.1 %all-to-all-start.1 = ((bf16[32,180,256]{2,1,0:T(8,128)(2,1)}), bf16[32,180,256]{2,1,0:T(8,128)(2,1)S(1)}, u32[]{:S(2)}, u32[]{:S(2)}) async-start(bf16[32,180,256]{2,1,0:T(8,128)(2,1)} %reshape.201), calls=%async_computation.2 | async-start | bytes 6029312 | tf_op jit(solution)/shard_map/all_to_all | solution.py:233
  177.4 0.0 reduce-scatter.7.cloned.1.call-start
  177.5 9.5 %fusion.1 = bf16[1280,1280]{0,1:T(8,128)(2,1)} fusion(bf16[1536,1280]{1,0:T(8,128)(2,1)} %get-tuple-element.14, bf16[1536,1280]{1,0:T(8,128)(2,1)} %memory_ref.1), kind=kOutput, calls=%fused_computation.3 | convolution fusion | flops 5034803200 | bytes 11141120 | tf_op jit(solution)/shard_map/dot_general | solution.py:212
  187.0 5.7 %copy.21 = bf16[1280,1280]{1,0:T(8,128)(2,1)} copy(bf16[1280,1280]{0,1:T(8,128)(2,1)} %fusion.1) | data formatting | bytes 6553600
  192.6 0.0 reduce-scatter.7.cloned.1.call-update
  192.6 0.1 reduce
  192.7 0.8 reshape.199.refs_0_
  193.5 54.4 %reduce-scatter.7.cloned.1.call-done = bf16[160,1280]{1,0:T(8,128)(2,1)} async-done(((bf16[1280,1280]{1,0:T(8,128)(2,1)}), bf16[160,1280]{1,0:T(8,128)(2,1)}) %reduce-scatter.7.cloned.1.call-update) | async-done | bytes 409616
  247.9 2.1 copy.22
  250.0 2.2 fusion.22
  252.2 2.0 copy.19
  254.3 2.0 copy.20
  256.3 0.0 all-to-all-done.1
  256.3 2.3 reshape.202.refs_1_
  258.6 13.1 %combine.1 = (f32[2048,256]{1,0:T(8,128)}, f32[2048,256]{1,0:T(8,128)}, f32[2048,256]{1,0:T(8,128)}) custom-call(s32[1,5760]{1,0:T(1,128)} %reshape.199.refs_0_, bf16[5760,256]{1,0:T(8,128)(2,1)} %reshape.202.refs_1_, f32[2048,256]{1,0:T(8,128)} %refs_2_.3, f32[2048,256]{1,0:T(8,128)} %refs_3_.1, f32[2048,256]{1,0:T(8,128)} %refs_4_.1), custom_call_target="tpu_custom_call" | custom-call | flops 6039797760 | bytes 12582912 | tf_op jit(solution)/shard_map/combine/pallas_call | solution.py:244
  (4 shorter events, 0.0 us)
Async XLA Ops:
  7.2 38.8 %all-gather.3.cloned.1.call-start = ((), (), s32[]{:S(2)}) async-start(), calls=%async_computation.4 | async-start | bytes 3686400 | tf_op jit(solution)/shard_map/all_gather | solution.py:142
  9.0 147.1 %reduce-scatter.5.cloned.1.call-start = ((), (), s32[]{:S(2)}) async-start(), calls=%async_computation.5 | async-start | bytes 4915200 | tf_op jit(solution)/shard_map/reduce_scatter | solution.py:210
  88.6 83.7 %all-to-all-start = ((s32[32,1,180]{2,1,0:T(1,128)}), s32[32,1,180]{2,1,0:T(1,128)S(1)}, u32[]{:S(2)}, u32[]{:S(2)}) async-start(s32[32,1,180]{2,1,0:T(1,128)} %copy.18), calls=%async_computation | async-start | bytes 65536 | tf_op jit(solution)/shard_map/all_to_all | solution.py:168
  172.3 84.0 %all-to-all-start.1 = ((bf16[32,180,256]{2,1,0:T(8,128)(2,1)}), bf16[32,180,256]{2,1,0:T(8,128)(2,1)S(1)}, u32[]{:S(2)}, u32[]{:S(2)}) async-start(bf16[32,180,256]{2,1,0:T(8,128)(2,1)} %reshape.201), calls=%async_computation.2 | async-start | bytes 6029312 | tf_op jit(solution)/shard_map/all_to_all | solution.py:233
  177.4 70.5 %reduce-scatter.7.cloned.1.call-start = ((), (), s32[]{:S(2)}) async-start(), calls=%async_computation.6 | async-start | bytes 3686400
Sparse Core Ops, SparseCore 0:
  10.4 35.4 all-gather.2
  83.8 72.2 reduce-scatter.4
  192.8 55.1 reduce-scatter.6
